TPU v7x, 32 devices: a whole 2x2x4 slice. The times are simulated.
32 devices in a mesh: col: 8 (over y, x, core), row: 4 (over z).
Axes of the slice: x: 2, y: 2, z: 4, core: 2. Of those that a mesh axis runs over, the one named last changes fastest.
Arguments:
- features: bfloat16 [65536, 2048], P(('col', 'row')), may hold values from -6 to 6
- leaf_in: bfloat16 [65536, 128], P(('col', 'row')), may hold values from -0.1875 to 0.1875
- mix_in: bfloat16 [3, 64, 128, 256], P(None, ('col', 'row')), may hold values from -0.375 to 0.375
- mix_out: bfloat16 [3, 64, 128, 256], P(None, 'col'), may hold values from -0.375 to 0.375
- leaf_out: bfloat16 [65536, 128], P('col'), may hold values from -0.5 to 0.5
Outputs:
- result: bfloat16 [65536, 2048], P(('col', 'row'))
All inputs are finite; a program needn't handle non-finite values.
Results may differ from a plain program's by a relative error of at most 0.023.
Values may be sent and summed in bfloat16 or wider, within the bound.
No kernel may reach another device: no remote copies, remote signals or barrier semaphores. Data moves between devices by JAX's collectives and lax.ppermute only.
A program may use at most 128 MiB of HBM per device.

v0:
```python
import jax
import jax.numpy as jnp
from jax import lax
from jax.sharding import PartitionSpec as P

LEAF_SIZE = 1024


def swapped(block, axis, stride):
    count = lax.axis_size(axis)
    route = []
    for low in range(count):
        high = low | 1 << stride
        if high != low and high < count:
            route += [(low, high), (high, low)]
    return lax.ppermute(block, axis, route)


def partner_of(coeffs, level_bit):
    total_blocks = coeffs.shape[0]
    shaped = coeffs.reshape(
        (total_blocks // (2 << level_bit), 2, 1 << level_bit) + coeffs.shape[1:]
    )
    return jnp.flip(shaped, 1).reshape(coeffs.shape)


def forward_mix(weights, coeffs, partner):
    stacked = jnp.concatenate([coeffs, partner], axis=1)
    return jnp.einsum("bkj,bjr->bkr", weights, stacked, preferred_element_type=jnp.float32).astype(
        jnp.bfloat16
    )


def backward_terms(weights, gradient):
    rank_size = gradient.shape[1]
    direct = jnp.einsum(
        "bjk,bjr->bkr", weights[:, :, :rank_size], gradient, preferred_element_type=jnp.float32
    )
    crossed = jnp.einsum(
        "bjk,bjr->bkr", weights[:, :, rank_size:], gradient, preferred_element_type=jnp.float32
    )
    return (direct, crossed.astype(jnp.bfloat16))


def body(features, leaf_in, mix_in, mix_out, leaf_out):
    rank_size = leaf_in.shape[1]
    side_count = features.shape[1]
    blocks = features.shape[0] // LEAF_SIZE
    col_bits = lax.axis_size("col").bit_length() - 1
    row_bits = lax.axis_size("row").bit_length() - 1
    feature_blocks = features.reshape(blocks, LEAF_SIZE, side_count)
    leaf_rows = leaf_in.reshape(blocks, LEAF_SIZE, rank_size)
    coeffs = jnp.einsum(
        "bmk,bmr->bkr", leaf_rows, feature_blocks, preferred_element_type=jnp.float32
    ).astype(jnp.bfloat16)
    for level_bit in range(col_bits):
        partner = swapped(coeffs, "col", level_bit)
        coeffs = forward_mix(mix_in[level_bit], coeffs, partner)
    coeffs = lax.all_to_all(coeffs, "row", split_axis=2, concat_axis=0, tiled=True)
    for level_bit in range(row_bits + 1):
        coeffs = forward_mix(mix_out[level_bit], coeffs, partner_of(coeffs, level_bit))
    out_rows = leaf_out.reshape(-1, LEAF_SIZE, rank_size)
    images = jnp.einsum(
        "bmk,bkr->bmr", out_rows, coeffs, preferred_element_type=jnp.float32
    ).astype(jnp.bfloat16)
    gradient = jnp.einsum(
        "bmk,bmr->bkr", out_rows, images, preferred_element_type=jnp.float32
    ).astype(jnp.bfloat16)
    for level_bit in reversed(range(row_bits + 1)):
        direct, crossed = backward_terms(mix_out[level_bit], gradient)
        gradient = (direct + partner_of(crossed, level_bit)).astype(jnp.bfloat16)
    gradient = lax.all_to_all(gradient, "row", split_axis=0, concat_axis=2, tiled=True)
    for level_bit in reversed(range(col_bits)):
        direct, crossed = backward_terms(mix_in[level_bit], gradient)
        gradient = (direct + swapped(crossed, "col", level_bit)).astype(jnp.bfloat16)
    result = jnp.einsum(
        "bmk,bkr->bmr", leaf_rows, gradient, preferred_element_type=jnp.float32
    ).astype(jnp.bfloat16)
    return result.reshape(features.shape)


def solution(mesh):
    in_specs = (
        P(("col", "row"), None),
        P(("col", "row"), None),
        P(None, ("col", "row"), None, None),
        P(None, "col", None, None),
        P("col", None),
    )
    out_specs = P(("col", "row"), None)
    return jax.shard_map(body, mesh=mesh, in_specs=in_specs, out_specs=out_specs, check_vma=False)
```

profile of v0, /device:TPU:0, one launch (start us, length us, event | category | flops | bytes accessed | tf_op | source)
XLA Modules:
  0.0 228.1 jit_solution(17529232885362974164)
XLA Ops:
  0.0 5.0 %convolution_convert_fusion.7 = bf16[2,128,2048]{2,1,0:T(8,128)(2,1)S(1)} fusion(bf16[2,1024,128]{2,1,0:T(8,128)(2,1)} %bitcast.112, bf16[2,1024,2048]{2,1,0:T(8,128)(2,1)} %bitcast.109), kind=kOutput, calls=%fused_computation.15 | convolution fusion | flops 1074266112 | bytes 9961472 | tf_op jit(solution)/shard_map/bmk,bmr->bkr/dot_general | solution.py:53
  5.0 0.6 collective-permute-start
  5.6 2.3 %collective-permute-done = bf16[2,128,2048]{2,1,0:T(8,128)(2,1)S(1)} collective-permute-done((bf16[2,128,2048]{2,1,0:T(8,128)(2,1)S(1)}, bf16[2,128,2048]{2,1,0:T(8,128)(2,1)S(1)}, u32[]{:S(2)}, u32[]{:S(2)}) %collective-permute-start) | collective-permute-done | bytes 1048608 | tf_op jit(solution)/shard_map/ppermute | solution.py:16
  7.9 0.5 fusion.10
  8.3 2.9 %collective-permute-start.1 = (bf16[2,128,2048]{2,1,0:T(8,128)(2,1)S(1)}, bf16[2,128,2048]{2,1,0:T(8,128)(2,1)S(1)}, u32[]{:S(2)}, u32[]{:S(2)}) collective-permute-start(bf16[2,128,2048]{2,1,0:T(8,128)(2,1)S(1)} %fusion.10), channel_id=1, source_target_pairs={{0,8},{8,0},{4,12},{12,4},{16,24},{24,16},{20,28},{28,20},{1,9},{9... | collective-permute-start | bytes 3145736 | tf_op jit(solution)/shard_map/ppermute | solution.py:16
  11.2 23.5 %collective-permute-done.1 = bf16[2,128,2048]{2,1,0:T(8,128)(2,1)S(1)} collective-permute-done((bf16[2,128,2048]{2,1,0:T(8,128)(2,1)S(1)}, bf16[2,128,2048]{2,1,0:T(8,128)(2,1)S(1)}, u32[]{:S(2)}, u32[]{:S(2)}) %collective-permute-start.1) | collective-permute-done | bytes 1048608 | tf_op jit(solution)/shard_map/ppermute | solution.py:16
  34.7 0.5 fusion.11
  35.2 1.8 collective-permute-start.2
  37.0 22.9 %collective-permute-done.2 = bf16[2,128,2048]{2,1,0:T(8,128)(2,1)S(1)} collective-permute-done((bf16[2,128,2048]{2,1,0:T(8,128)(2,1)S(1)}, bf16[2,128,2048]{2,1,0:T(8,128)(2,1)S(1)}, u32[]{:S(2)}, u32[]{:S(2)}) %collective-permute-start.2) | collective-permute-done | bytes 1048608 | tf_op jit(solution)/shard_map/ppermute | solution.py:16
  59.9 0.9 fusion.9
  60.8 9.5 %copy.13 = bf16[2,128,2048]{1,0,2:T(2,128)(2,1)} copy(bf16[2,128,2048]{1,2,0:T(8,128)(2,1)S(1)} %fusion.9) | data formatting | bytes 2097152 | tf_op jit(solution)/shard_map/convert_element_type | solution.py:29
  70.3 4.8 %all-to-all-start = ((bf16[2,128,2048]{1,0,2:T(2,128)(2,1)}), bf16[2,128,2048]{1,0,2:T(2,128)(2,1)S(1)}, u32[]{:S(2)}, u32[]{:S(2)}) async-start(bf16[2,128,2048]{1,0,2:T(2,128)(2,1)} %copy.13), calls=%async_computation | async-start | bytes 2097152 | tf_op jit(solution)/shard_map/all_to_all | solution.py:59
  75.1 2.6 %slice_bitcast_fusion.2 = (bf16[8,128,256]{2,1,0:T(8,128)(2,1)}, bf16[8,128,256]{2,1,0:T(8,128)(2,1)}, bf16[8,128,256]{2,1,0:T(8,128)(2,1)}) fusion(bf16[3,8,128,256]{3,2,1,0:T(8,128)(2,1)} %param.8), kind=kLoop, calls=%fused_computation.60 | loop fusion | bytes 3145728 | tf_op jit(solution)/shard_map/squeeze | solution.py:70
  77.7 21.8 %all-to-all-done = bf16[2,128,2048]{1,0,2:T(2,128)(2,1)S(1)} async-done(((bf16[2,128,2048]{1,0,2:T(2,128)(2,1)}), bf16[2,128,2048]{1,0,2:T(2,128)(2,1)S(1)}, u32[]{:S(2)}, u32[]{:S(2)}) %all-to-all-start) | async-done | bytes 1048608 | tf_op jit(solution)/shard_map/all_to_all | solution.py:59
  99.4 2.0 copy.14
  101.4 2.4 %reverse.3 = bf16[4,2,128,512]{3,2,1,0:T(8,128)(2,1)} reverse(bf16[4,2,128,512]{3,2,1,0:T(8,128)(2,1)} %bitcast.119), dimensions={1} | reverse | bytes 2097152 | tf_op jit(solution)/shard_map/reverse
  103.8 2.8 %fusion.42 = bf16[8,512,128]{1,2,0:T(8,128)(2,1)} fusion(bf16[8,128,512]{2,1,0:T(8,128)(2,1)} %bitcast.128, bf16[8,128,512]{2,1,0:T(8,128)(2,1)S(1)} %bitcast.120, bf16[3,8,128,256]{3,2,1,0:T(8,128)(2,1)} %param.8), kind=kOutput, calls=%fused_computation.53 | convolution fusion | flops 273154048 | bytes 3670016 | tf_op jit(solution)/shard_map/bkj,bjr->bkr/dot_general | solution.py:29
  106.6 2.4 %rev.19 = bf16[2,2,2,128,512]{4,3,2,1,0:T(8,128)(2,1)} reverse(bf16[2,2,2,128,512]{4,3,2,1,0:T(8,128)(2,1)} %bitcast.124), dimensions={1} | reverse | bytes 2097152 | tf_op jit(solution)/shard_map/jit(_flip)/rev | solution.py:24
  108.9 2.8 %fusion.39 = bf16[8,512,128]{1,2,0:T(8,128)(2,1)} fusion(bf16[8,128,512]{2,1,0:T(8,128)(2,1)} %bitcast.129, bf16[8,128,512]{2,1,0:T(8,128)(2,1)S(1)} %bitcast.125, bf16[3,8,128,256]{3,2,1,0:T(8,128)(2,1)} %param.8), kind=kOutput, calls=%fused_computation.52 | convolution fusion | flops 273154048 | bytes 3670016 | tf_op jit(solution)/shard_map/bkj,bjr->bkr/dot_general | solution.py:29
  111.8 2.4 %rev.20 = bf16[1,2,4,128,512]{4,3,2,1,0:T(8,128)(2,1)} reverse(bf16[1,2,4,128,512]{4,3,2,1,0:T(8,128)(2,1)} %bitcast.126), dimensions={1} | reverse | bytes 2097152 | tf_op jit(solution)/shard_map/jit(_flip)/rev | solution.py:24
  114.1 3.2 %fusion.36 = bf16[8,512,128]{2,1,0:T(8,128)(2,1)} fusion(bf16[8,128,512]{2,1,0:T(8,128)(2,1)} %bitcast.130, bf16[8,128,512]{2,1,0:T(8,128)(2,1)S(1)} %bitcast.127, bf16[3,8,128,256]{3,2,1,0:T(8,128)(2,1)} %param.8), kind=kOutput, calls=%fused_computation.51 | convolution fusion | flops 273154048 | bytes 3670016 | tf_op jit(solution)/shard_map/bkj,bjr->bkr/dot_general | solution.py:29
  117.3 5.7 %fusion.45 = bf16[8,512,128]{2,1,0:T(8,128)(2,1)S(1)} fusion(bf16[8,1024,128]{2,1,0:T(8,128)(2,1)S(1)} %bitcast.108, bf16[8,512,128]{2,1,0:T(8,128)(2,1)} %fusion.36), kind=kOutput, calls=%fused_computation.54 | convolution fusion | flops 2152202240 | bytes 4194304 | tf_op jit(solution)/shard_map/bmk,bmr->bkr/dot_general | solution.py:66
  123.0 2.3 %convolution_convert_fusion.10 = bf16[8,512,128]{2,1,0:T(8,128)(2,1)} fusion(bf16[8,512,128]{2,1,0:T(8,128)(2,1)S(1)} %fusion.45, bf16[8,128,256]{2,1,0:T(8,128)(2,1)} %get-tuple-element.6), kind=kOutput, calls=%fused_computation.57 | convolution fusion | flops 134742016 | bytes 2359296 | tf_op jit(solution)/shard_map/bjk,bjr->bkr/dot_general | solution.py:39
  125.4 2.3 rev.21
  127.6 1.8 fusion.35
  129.4 1.0 copy-done.1
  130.4 0.4 convolution_convert_fusion.9
  130.8 1.0 rev.22
  131.9 2.1 fusion.34
  134.0 1.4 convolution_convert_fusion.8
  135.4 2.3 rev.23
  137.7 2.7 %fusion.33 = bf16[8,128,512]{1,2,0:T(8,128)(2,1)} fusion(bf16[8,128,512]{1,2,0:T(8,128)(2,1)} %bitcast.118, bf16[8,128,512]{1,2,0:T(8,128)(2,1)S(1)} %fusion.34, bf16[8,128,256]{2,1,0:T(8,128)(2,1)} %get-tuple-element.5), kind=kOutput, calls=%fused_computation.44 | convolution fusion | flops 135790592 | bytes 3407872 | tf_op jit(solution)/shard_map/bjk,bjr->bkr/dot_general | solution.py:36
  140.4 3.7 %all-to-all-start.1 = ((bf16[8,128,512]{1,2,0:T(8,128)(2,1)}), bf16[8,128,512]{1,2,0:T(8,128)(2,1)S(1)}, u32[]{:S(2)}, u32[]{:S(2)}) async-start(bf16[8,128,512]{1,2,0:T(8,128)(2,1)} %fusion.33), calls=%async_computation.1 | async-start | bytes 2097152 | tf_op jit(solution)/shard_map/all_to_all | solution.py:72
  144.1 1.1 slice_bitcast_fusion.5
  145.2 24.0 %all-to-all-done.1 = bf16[8,128,512]{1,2,0:T(8,128)(2,1)S(1)} async-done(((bf16[8,128,512]{1,2,0:T(8,128)(2,1)}), bf16[8,128,512]{1,2,0:T(8,128)(2,1)S(1)}, u32[]{:S(2)}, u32[]{:S(2)}) %all-to-all-start.1) | async-done | bytes 1048608 | tf_op jit(solution)/shard_map/all_to_all | solution.py:72
  169.2 0.1 copy.15
  169.2 0.4 fusion.6
  169.7 1.6 collective-permute-start.3
  171.3 22.6 %collective-permute-done.3 = bf16[2,128,2048]{1,2,0:T(8,128)(2,1)S(1)} collective-permute-done((bf16[2,128,2048]{1,2,0:T(8,128)(2,1)S(1)}, bf16[2,128,2048]{1,2,0:T(8,128)(2,1)S(1)}, u32[]{:S(2)}, u32[]{:S(2)}) %collective-permute-start.3) | collective-permute-done | bytes 1048608 | tf_op jit(solution)/shard_map/ppermute | solution.py:16
  193.9 0.4 add_convert_fusion.1
  194.3 0.4 fusion.7
  194.7 1.6 collective-permute-start.4
  196.3 21.8 %collective-permute-done.4 = bf16[2,128,2048]{1,2,0:T(8,128)(2,1)S(1)} collective-permute-done((bf16[2,128,2048]{1,2,0:T(8,128)(2,1)S(1)}, bf16[2,128,2048]{1,2,0:T(8,128)(2,1)S(1)}, u32[]{:S(2)}, u32[]{:S(2)}) %collective-permute-start.4) | collective-permute-done | bytes 1048608 | tf_op jit(solution)/shard_map/ppermute | solution.py:16
  218.1 0.4 fusion.5
  218.5 0.5 fusion.8
  219.0 0.1 collective-permute-start.5
  219.1 2.8 %collective-permute-done.5 = bf16[2,128,2048]{2,1,0:T(8,128)(2,1)} collective-permute-done((bf16[2,128,2048]{2,1,0:T(8,128)(2,1)S(1)}, bf16[2,128,2048]{2,1,0:T(8,128)(2,1)}, u32[]{:S(2)}, u32[]{:S(2)}) %collective-permute-start.5) | collective-permute-done | bytes 1048608 | tf_op jit(solution)/shard_map/ppermute | solution.py:16
  221.9 6.2 %convolution_convert_fusion = bf16[2,2048,1024]{1,2,0:T(8,128)(2,1)} fusion(bf16[2,1024,128]{2,1,0:T(8,128)(2,1)} %bitcast.113, bf16[2,128,2048]{2,1,0:T(8,128)(2,1)} %collective-permute-done.5, bf16[2,128,2048]{1,2,0:T(8,128)(2,1)S(1)} %fusion.5, bf16[2,128,256]{2,1,0:T(8,128)(2,1)S(1)} %get-tuple-element.8), kind=kOutput, calls=%fused_computation.2 | convolution fusion | flops 1213726720 | bytes 11075584 | tf_op jit(solution)/shard_map/bmk,bkr->bmr/dot_general | solution.py:76
  (15 shorter events, 0.0 us)
Async XLA Ops:
  0.0 117.3 %copy-start = (bf16[8192,128]{1,0:T(8,128)(2,1)S(1)}, bf16[8192,128]{1,0:T(8,128)(2,1)}, u32[]{:S(2)}) copy-start(bf16[8192,128]{1,0:T(8,128)(2,1)} %param.9) | copy-start | bytes 6291460
  0.0 7.9 %copy-start.7 = (bf16[3,2,128,256]{3,2,1,0:T(8,128)(2,1)S(1)}, bf16[3,2,128,256]{3,2,1,0:T(8,128)(2,1)}, u32[]{:S(2)}) copy-start(bf16[3,2,128,256]{3,2,1,0:T(8,128)(2,1)} %param.7) | copy-start | bytes 1179652
  5.0 2.8 %collective-permute-start = (bf16[2,128,2048]{2,1,0:T(8,128)(2,1)S(1)}, bf16[2,128,2048]{2,1,0:T(8,128)(2,1)S(1)}, u32[]{:S(2)}, u32[]{:S(2)}) collective-permute-start(bf16[2,128,2048]{2,1,0:T(8,128)(2,1)S(1)} %convolution_convert_fusion.7), channel_id=1, source_target_pairs={{0,4},{4,0},{8,12},{12,8},{16,20},{20,16},{24,28},{28,24},{1,5},{5... | collective-permute-start | bytes 3145736 | tf_op jit(solution)/shard_map/ppermute | solution.py:16
  8.3 26.4 %collective-permute-start.1 = (bf16[2,128,2048]{2,1,0:T(8,128)(2,1)S(1)}, bf16[2,128,2048]{2,1,0:T(8,128)(2,1)S(1)}, u32[]{:S(2)}, u32[]{:S(2)}) collective-permute-start(bf16[2,128,2048]{2,1,0:T(8,128)(2,1)S(1)} %fusion.10), channel_id=1, source_target_pairs={{0,8},{8,0},{4,12},{12,4},{16,24},{24,16},{20,28},{28,20},{1,9},{9... | collective-permute-start | bytes 3145736 | tf_op jit(solution)/shard_map/ppermute | solution.py:16
  35.2 24.7 %collective-permute-start.2 = (bf16[2,128,2048]{2,1,0:T(8,128)(2,1)S(1)}, bf16[2,128,2048]{2,1,0:T(8,128)(2,1)S(1)}, u32[]{:S(2)}, u32[]{:S(2)}) collective-permute-start(bf16[2,128,2048]{2,1,0:T(8,128)(2,1)S(1)} %fusion.11), channel_id=1, source_target_pairs={{0,16},{16,0},{4,20},{20,4},{8,24},{24,8},{12,28},{28,12},{1,17},{... | collective-permute-start | bytes 3145736 | tf_op jit(solution)/shard_map/ppermute | solution.py:16
  70.3 29.2 %all-to-all-start = ((bf16[2,128,2048]{1,0,2:T(2,128)(2,1)}), bf16[2,128,2048]{1,0,2:T(2,128)(2,1)S(1)}, u32[]{:S(2)}, u32[]{:S(2)}) async-start(bf16[2,128,2048]{1,0,2:T(2,128)(2,1)} %copy.13), calls=%async_computation | async-start | bytes 2097152 | tf_op jit(solution)/shard_map/all_to_all | solution.py:59
  101.4 2.4 %copy-start.2 = (bf16[2,128,4,512]{3,1,0,2:T(8,128)(2,1)S(1)}, bf16[2,128,4,512]{3,1,0,2:T(8,128)(2,1)}, u32[]{:S(2)}) copy-start(bf16[2,128,4,512]{3,1,0,2:T(8,128)(2,1)} %copy.14) | copy-start | bytes 3145732
  106.6 2.4 %copy-start.5 = (bf16[8,512,128]{1,2,0:T(8,128)(2,1)S(1)}, bf16[8,512,128]{1,2,0:T(8,128)(2,1)}, u32[]{:S(2)}) copy-start(bf16[8,512,128]{1,2,0:T(8,128)(2,1)} %fusion.42) | copy-start | bytes 3145732
  111.8 2.4 %copy-start.6 = (bf16[8,512,128]{1,2,0:T(8,128)(2,1)S(1)}, bf16[8,512,128]{1,2,0:T(8,128)(2,1)}, u32[]{:S(2)}) copy-start(bf16[8,512,128]{1,2,0:T(8,128)(2,1)} %fusion.39) | copy-start | bytes 3145732
  127.6 2.8 %copy-start.4 = (bf16[8,128,256]{2,1,0:T(8,128)(2,1)S(1)}, bf16[8,128,256]{2,1,0:T(8,128)(2,1)}, u32[]{:S(2)}) copy-start(bf16[8,128,256]{2,1,0:T(8,128)(2,1)} %get-tuple-element.7) | copy-start | bytes 1572868
  129.4 1.0 copy-start.1
  131.9 2.1 copy-start.3
  140.4 28.8 %all-to-all-start.1 = ((bf16[8,128,512]{1,2,0:T(8,128)(2,1)}), bf16[8,128,512]{1,2,0:T(8,128)(2,1)S(1)}, u32[]{:S(2)}, u32[]{:S(2)}) async-start(bf16[8,128,512]{1,2,0:T(8,128)(2,1)} %fusion.33), calls=%async_computation.1 | async-start | bytes 2097152 | tf_op jit(solution)/shard_map/all_to_all | solution.py:72
  169.7 24.2 %collective-permute-start.3 = (bf16[2,128,2048]{1,2,0:T(8,128)(2,1)S(1)}, bf16[2,128,2048]{1,2,0:T(8,128)(2,1)S(1)}, u32[]{:S(2)}, u32[]{:S(2)}) collective-permute-start(bf16[2,128,2048]{1,2,0:T(8,128)(2,1)S(1)} %fusion.6), channel_id=1, source_target_pairs={{0,16},{16,0},{4,20},{20,4},{8,24},{24,8},{12,28},{28,12},{1,17},{... | collective-permute-start | bytes 3145736 | tf_op jit(solution)/shard_map/ppermute | solution.py:16
  194.7 23.4 %collective-permute-start.4 = (bf16[2,128,2048]{1,2,0:T(8,128)(2,1)S(1)}, bf16[2,128,2048]{1,2,0:T(8,128)(2,1)S(1)}, u32[]{:S(2)}, u32[]{:S(2)}) collective-permute-start(bf16[2,128,2048]{1,2,0:T(8,128)(2,1)S(1)} %fusion.7), channel_id=1, source_target_pairs={{0,8},{8,0},{4,12},{12,4},{16,24},{24,16},{20,28},{28,20},{1,9},{9... | collective-permute-start | bytes 3145736 | tf_op jit(solution)/shard_map/ppermute | solution.py:16
  219.0 2.9 %collective-permute-start.5 = (bf16[2,128,2048]{2,1,0:T(8,128)(2,1)S(1)}, bf16[2,128,2048]{2,1,0:T(8,128)(2,1)}, u32[]{:S(2)}, u32[]{:S(2)}) collective-permute-start(bf16[2,128,2048]{2,1,0:T(8,128)(2,1)S(1)} %fusion.8), channel_id=1, source_target_pairs={{0,4},{4,0},{8,12},{12,8},{16,20},{20,16},{24,28},{28,24},{1,5},{5... | collective-permute-start | bytes 3145736 | tf_op jit(solution)/shard_map/ppermute | solution.py:16
where the time goes:
time: 229 us; the launch traced here: 228 us
  waiting for transfers between devices  142 us (62%)
  matrix products  40.4 us (18%)
  local copies, waits for them, and re-layouts  28.8 us (13%)
  starting transfers between devices  17.1 us (7%)
    ppermute x6, waiting for transfers between devices, swapped(): return lax.ppermute(block, axis, route)  95.8 us
    all_to_all x1, waiting for transfers between devices, body(): lax.all_to_all(gradient, 'row', split_axis=0, concat_axis=2, tiled=True)  24 us
    all_to_all x1, waiting for transfers between devices, body(): lax.all_to_all(coeffs, 'row', split_axis=2, concat_axis=0, tiled=True)  21.8 us
    dot_general x6, matrix products, forward_mix(): jnp.einsum('bkj,bjr->bkr', weights, stacked, preferred_element_type=jnp.f...  10.6 us
    rev x5, local copies, waits for them, and re-layouts, partner_of(): return jnp.flip(shaped, 1).reshape(coeffs.shape)  10.3 us
    convert_element_type x1, local copies, waits for them, and re-layouts, forward_mix(): jnp.einsum('bkj,bjr->bkr', weights, stacked, preferred_element_type=jnp.f...  9.46 us
    ppermute x6, starting transfers between devices, swapped(): return lax.ppermute(block, axis, route)  8.57 us
    dot_general x5, matrix products, backward_terms(): jnp.einsum('bjk,bjr->bkr', weights[:, :, :rank_size], gradient, preferred...  7.42 us
  transfers between devices with their start and end apart: 8, of which 8 were waited for; matrix products, arithmetic and copies ran while one was open for 2% of the time, Pallas kernels for 0%

commit v1 on v0

--- a/solution.py
+++ b/solution.py
@@ -56,7 +56,10 @@
     for level_bit in range(col_bits):
         partner = swapped(coeffs, "col", level_bit)
         coeffs = forward_mix(mix_in[level_bit], coeffs, partner)
-    coeffs = lax.all_to_all(coeffs, "row", split_axis=2, concat_axis=0, tiled=True)
+    coeffs = jnp.concatenate(
+        lax.all_to_all(jnp.stack(jnp.split(coeffs, lax.axis_size("row"), axis=2)), "row", 0, 0),
+        axis=0,
+    )
     for level_bit in range(row_bits + 1):
         coeffs = forward_mix(mix_out[level_bit], coeffs, partner_of(coeffs, level_bit))
     out_rows = leaf_out.reshape(-1, LEAF_SIZE, rank_size)

time: 229 us -> 221 us (0.965)
  local copies, waits for them, and re-layouts: 28.8 us -> 19.8 us
    convert_element_type x1 -> x0, local copies, waits for them, and re-layouts: 9.46 us -> none  [forward_mix(): jnp.einsum('bkj,bjr->bkr', weights, stacked, preferred_element_type=jnp.f...]
    reshape x0 -> x2, local copies, waits for them, and re-layouts: none -> 3.69 us  [the longest x1 2.35 us: partner_of(): return jnp.flip(shaped, 1).reshape(coeffs.shape)]
where the time goes in v1:
time: 221 us; the launch traced here: 220 us
  waiting for transfers between devices  142 us (64%)
  matrix products  40.4 us (18%)
  local copies, waits for them, and re-layouts  19.8 us (9%)
  starting transfers between devices  17.1 us (8%)
    ppermute x6, waiting for transfers between devices, swapped(): return lax.ppermute(block, axis, route)  95.8 us
    all_to_all x1, waiting for transfers between devices, body(): lax.all_to_all(gradient, 'row', split_axis=0, concat_axis=2, tiled=True)  24 us
    all_to_all x1, waiting for transfers between devices, body(): lax.all_to_all(jnp.stack(jnp.split(coeffs, lax.axis_size('row'), axis=2))...  21.8 us
    dot_general x6, matrix products, forward_mix(): jnp.einsum('bkj,bjr->bkr', weights, stacked, preferred_element_type=jnp.f...  10.6 us
    rev x5, local copies, waits for them, and re-layouts, partner_of(): return jnp.flip(shaped, 1).reshape(coeffs.shape)  10.4 us
    ppermute x6, starting transfers between devices, swapped(): return lax.ppermute(block, axis, route)  8.54 us
    dot_general x5, matrix products, backward_terms(): jnp.einsum('bjk,bjr->bkr', weights[:, :, :rank_size], gradient, preferred...  7.42 us
    dot_general x1, matrix products, body(): jnp.einsum('bmk,bkr->bmr', leaf_rows, gradient, preferred_element_type=jn...  6.18 us
  transfers between devices with their start and end apart: 8, of which 8 were waited for; matrix products, arithmetic and copies ran while one was open for 2% of the time, Pallas kernels for 0%

profile of v1, /device:TPU:0, one launch (start us, length us, event | category | flops | bytes accessed | tf_op | source)
XLA Modules:
  0.0 220.2 jit_solution(18189421913028967174)
XLA Ops:
  0.0 5.0 %convolution_convert_fusion.7 = bf16[2,128,2048]{2,1,0:T(8,128)(2,1)S(1)} fusion(bf16[2,1024,128]{2,1,0:T(8,128)(2,1)} %bitcast.118, bf16[2,1024,2048]{2,1,0:T(8,128)(2,1)} %bitcast.114), kind=kOutput, calls=%fused_computation.15 | convolution fusion | flops 1074266112 | bytes 9961472 | tf_op jit(solution)/shard_map/bmk,bmr->bkr/dot_general | solution.py:53
  5.0 0.6 collective-permute-start
  5.6 2.3 %collective-permute-done = bf16[2,128,2048]{2,1,0:T(8,128)(2,1)S(1)} collective-permute-done((bf16[2,128,2048]{2,1,0:T(8,128)(2,1)S(1)}, bf16[2,128,2048]{2,1,0:T(8,128)(2,1)S(1)}, u32[]{:S(2)}, u32[]{:S(2)}) %collective-permute-start) | collective-permute-done | bytes 1048608 | tf_op jit(solution)/shard_map/ppermute | solution.py:16
  7.9 0.5 fusion.10
  8.3 2.9 %collective-permute-start.1 = (bf16[2,128,2048]{2,1,0:T(8,128)(2,1)S(1)}, bf16[2,128,2048]{2,1,0:T(8,128)(2,1)S(1)}, u32[]{:S(2)}, u32[]{:S(2)}) collective-permute-start(bf16[2,128,2048]{2,1,0:T(8,128)(2,1)S(1)} %fusion.10), channel_id=1, source_target_pairs={{0,8},{8,0},{4,12},{12,4},{16,24},{24,16},{20,28},{28,20},{1,9},{9... | collective-permute-start | bytes 3145736 | tf_op jit(solution)/shard_map/ppermute | solution.py:16
  11.2 23.5 %collective-permute-done.1 = bf16[2,128,2048]{2,1,0:T(8,128)(2,1)S(1)} collective-permute-done((bf16[2,128,2048]{2,1,0:T(8,128)(2,1)S(1)}, bf16[2,128,2048]{2,1,0:T(8,128)(2,1)S(1)}, u32[]{:S(2)}, u32[]{:S(2)}) %collective-permute-start.1) | collective-permute-done | bytes 1048608 | tf_op jit(solution)/shard_map/ppermute | solution.py:16
  34.7 0.5 fusion.11
  35.2 1.8 collective-permute-start.2
  37.0 22.9 %collective-permute-done.2 = bf16[2,128,2048]{2,1,0:T(8,128)(2,1)S(1)} collective-permute-done((bf16[2,128,2048]{2,1,0:T(8,128)(2,1)S(1)}, bf16[2,128,2048]{2,1,0:T(8,128)(2,1)S(1)}, u32[]{:S(2)}, u32[]{:S(2)}) %collective-permute-start.2) | collective-permute-done | bytes 1048608 | tf_op jit(solution)/shard_map/ppermute | solution.py:16
  59.9 0.9 fusion.9
  60.9 1.1 pad_maximum_fusion
  62.0 4.8 %all-to-all-start = ((bf16[4,2,128,512]{2,3,1,0:T(8,128)(2,1)}), bf16[4,2,128,512]{2,3,1,0:T(8,128)(2,1)S(1)}, u32[]{:S(2)}, u32[]{:S(2)}) async-start(bf16[4,2,128,512]{2,3,1,0:T(8,128)(2,1)} %pad_maximum_fusion), calls=%async_computation | async-start | bytes 2097152 | tf_op jit(solution)/shard_map/all_to_all | solution.py:60
  66.8 2.5 %slice_bitcast_fusion.2 = (bf16[8,128,256]{2,1,0:T(8,128)(2,1)}, bf16[8,128,256]{2,1,0:T(8,128)(2,1)}, bf16[8,128,256]{2,1,0:T(8,128)(2,1)}) fusion(bf16[3,8,128,256]{3,2,1,0:T(8,128)(2,1)} %param.8), kind=kLoop, calls=%fused_computation.61 | loop fusion | bytes 3145728 | tf_op jit(solution)/shard_map/squeeze | solution.py:73
  69.4 21.8 %all-to-all-done = bf16[4,2,128,512]{2,3,1,0:T(8,128)(2,1)S(1)} async-done(((bf16[4,2,128,512]{2,3,1,0:T(8,128)(2,1)}), bf16[4,2,128,512]{2,3,1,0:T(8,128)(2,1)S(1)}, u32[]{:S(2)}, u32[]{:S(2)}) %all-to-all-start) | async-done | bytes 1048608 | tf_op jit(solution)/shard_map/all_to_all | solution.py:60
  91.1 1.3 copy.8
  92.5 1.0 reverse.3
  93.5 2.4 %copy.9 = bf16[8,128,512]{2,1,0:T(8,128)(2,1)} copy(bf16[8,128,512]{1,2,0:T(8,128)(2,1)} %bitcast.124) | data formatting | bytes 2097152 | tf_op jit(solution)/shard_map/reshape | solution.py:24
  95.9 2.8 %fusion.42 = bf16[8,512,128]{1,2,0:T(8,128)(2,1)} fusion(bf16[8,128,512]{2,1,0:T(8,128)(2,1)} %copy.9, bf16[8,128,512]{2,1,0:T(8,128)(2,1)S(1)} %copy-done.4, bf16[3,8,128,256]{3,2,1,0:T(8,128)(2,1)} %param.8), kind=kOutput, calls=%fused_computation.53 | convolution fusion | flops 273154048 | bytes 3670016 | tf_op jit(solution)/shard_map/bkj,bjr->bkr/dot_general | solution.py:29
  98.7 2.4 %rev.19 = bf16[2,2,2,128,512]{4,3,2,1,0:T(8,128)(2,1)} reverse(bf16[2,2,2,128,512]{4,3,2,1,0:T(8,128)(2,1)} %bitcast.128), dimensions={1} | reverse | bytes 2097152 | tf_op jit(solution)/shard_map/jit(_flip)/rev | solution.py:24
  101.1 2.8 %fusion.39 = bf16[8,512,128]{1,2,0:T(8,128)(2,1)} fusion(bf16[8,128,512]{2,1,0:T(8,128)(2,1)} %bitcast.132, bf16[8,128,512]{2,1,0:T(8,128)(2,1)S(1)} %bitcast.129, bf16[3,8,128,256]{3,2,1,0:T(8,128)(2,1)} %param.8), kind=kOutput, calls=%fused_computation.52 | convolution fusion | flops 273154048 | bytes 3670016 | tf_op jit(solution)/shard_map/bkj,bjr->bkr/dot_general | solution.py:29
  103.9 2.4 %rev.20 = bf16[1,2,4,128,512]{4,3,2,1,0:T(8,128)(2,1)} reverse(bf16[1,2,4,128,512]{4,3,2,1,0:T(8,128)(2,1)} %bitcast.130), dimensions={1} | reverse | bytes 2097152 | tf_op jit(solution)/shard_map/jit(_flip)/rev | solution.py:24
  106.3 3.2 %fusion.36 = bf16[8,512,128]{2,1,0:T(8,128)(2,1)} fusion(bf16[8,128,512]{2,1,0:T(8,128)(2,1)} %bitcast.133, bf16[8,128,512]{2,1,0:T(8,128)(2,1)S(1)} %bitcast.131, bf16[3,8,128,256]{3,2,1,0:T(8,128)(2,1)} %param.8), kind=kOutput, calls=%fused_computation.51 | convolution fusion | flops 273154048 | bytes 3670016 | tf_op jit(solution)/shard_map/bkj,bjr->bkr/dot_general | solution.py:29
  109.4 5.7 %fusion.45 = bf16[8,512,128]{2,1,0:T(8,128)(2,1)S(1)} fusion(bf16[8,1024,128]{2,1,0:T(8,128)(2,1)S(1)} %bitcast.113, bf16[8,512,128]{2,1,0:T(8,128)(2,1)} %fusion.36), kind=kOutput, calls=%fused_computation.54 | convolution fusion | flops 2152202240 | bytes 4194304 | tf_op jit(solution)/shard_map/bmk,bmr->bkr/dot_general | solution.py:69
  115.2 2.3 %convolution_convert_fusion.10 = bf16[8,512,128]{2,1,0:T(8,128)(2,1)} fusion(bf16[8,512,128]{2,1,0:T(8,128)(2,1)S(1)} %fusion.45, bf16[8,128,256]{2,1,0:T(8,128)(2,1)} %get-tuple-element.6), kind=kOutput, calls=%fused_computation.57 | convolution fusion | flops 134742016 | bytes 2359296 | tf_op jit(solution)/shard_map/bjk,bjr->bkr/dot_general | solution.py:39
  117.5 2.3 %rev.21 = bf16[1,2,4,128,512]{3,4,2,1,0:T(8,128)(2,1)} reverse(bf16[1,2,4,128,512]{3,4,2,1,0:T(8,128)(2,1)} %bitcast.125), dimensions={1} | reverse | bytes 2097152 | tf_op jit(solution)/shard_map/jit(_flip)/rev | solution.py:24
  119.8 1.8 fusion.35
  121.6 1.0 copy-done.1
  122.6 0.4 convolution_convert_fusion.9
  123.0 1.0 rev.22
  124.1 2.1 fusion.34
  126.2 1.4 convolution_convert_fusion.8
  127.6 2.3 %rev.23 = bf16[4,2,1,128,512]{3,4,1,0,2:T(8,128)(2,1)} reverse(bf16[4,2,1,128,512]{3,4,1,0,2:T(8,128)(2,1)} %bitcast.127), dimensions={1} | reverse | bytes 2097152 | tf_op jit(solution)/shard_map/jit(_flip)/rev | solution.py:24
  129.9 2.7 %fusion.33 = bf16[8,128,512]{1,2,0:T(8,128)(2,1)} fusion(bf16[8,128,512]{1,2,0:T(8,128)(2,1)} %bitcast.123, bf16[8,128,512]{1,2,0:T(8,128)(2,1)S(1)} %fusion.34, bf16[8,128,256]{2,1,0:T(8,128)(2,1)} %get-tuple-element.5), kind=kOutput, calls=%fused_computation.44 | convolution fusion | flops 135790592 | bytes 3407872 | tf_op jit(solution)/shard_map/bjk,bjr->bkr/dot_general | solution.py:36
  132.6 3.7 %all-to-all-start.1 = ((bf16[8,128,512]{1,2,0:T(8,128)(2,1)}), bf16[8,128,512]{1,2,0:T(8,128)(2,1)S(1)}, u32[]{:S(2)}, u32[]{:S(2)}) async-start(bf16[8,128,512]{1,2,0:T(8,128)(2,1)} %fusion.33), calls=%async_computation.1 | async-start | bytes 2097152 | tf_op jit(solution)/shard_map/all_to_all | solution.py:75
  136.3 1.1 slice_bitcast_fusion.9
  137.4 24.0 %all-to-all-done.1 = bf16[8,128,512]{1,2,0:T(8,128)(2,1)S(1)} async-done(((bf16[8,128,512]{1,2,0:T(8,128)(2,1)}), bf16[8,128,512]{1,2,0:T(8,128)(2,1)S(1)}, u32[]{:S(2)}, u32[]{:S(2)}) %all-to-all-start.1) | async-done | bytes 1048608 | tf_op jit(solution)/shard_map/all_to_all | solution.py:75
  161.4 0.4 fusion.6
  161.8 1.6 collective-permute-start.3
  163.4 22.7 %collective-permute-done.3 = bf16[2,128,2048]{1,2,0:T(8,128)(2,1)S(1)} collective-permute-done((bf16[2,128,2048]{1,2,0:T(8,128)(2,1)S(1)}, bf16[2,128,2048]{1,2,0:T(8,128)(2,1)S(1)}, u32[]{:S(2)}, u32[]{:S(2)}) %collective-permute-start.3) | collective-permute-done | bytes 1048608 | tf_op jit(solution)/shard_map/ppermute | solution.py:16
  186.1 0.4 add_convert_fusion.1
  186.5 0.4 fusion.7
  186.9 1.6 collective-permute-start.4
  188.5 21.8 %collective-permute-done.4 = bf16[2,128,2048]{1,2,0:T(8,128)(2,1)S(1)} collective-permute-done((bf16[2,128,2048]{1,2,0:T(8,128)(2,1)S(1)}, bf16[2,128,2048]{1,2,0:T(8,128)(2,1)S(1)}, u32[]{:S(2)}, u32[]{:S(2)}) %collective-permute-start.4) | collective-permute-done | bytes 1048608 | tf_op jit(solution)/shard_map/ppermute | solution.py:16
  210.3 0.4 fusion.5
  210.7 0.5 fusion.8
  211.2 0.1 collective-permute-start.5
  211.3 2.8 %collective-permute-done.5 = bf16[2,128,2048]{2,1,0:T(8,128)(2,1)} collective-permute-done((bf16[2,128,2048]{2,1,0:T(8,128)(2,1)S(1)}, bf16[2,128,2048]{2,1,0:T(8,128)(2,1)}, u32[]{:S(2)}, u32[]{:S(2)}) %collective-permute-start.5) | collective-permute-done | bytes 1048608 | tf_op jit(solution)/shard_map/ppermute | solution.py:16
  214.1 6.2 %convolution_convert_fusion = bf16[2,2048,1024]{1,2,0:T(8,128)(2,1)} fusion(bf16[2,1024,128]{2,1,0:T(8,128)(2,1)} %bitcast.119, bf16[2,128,2048]{2,1,0:T(8,128)(2,1)} %collective-permute-done.5, bf16[2,128,2048]{1,2,0:T(8,128)(2,1)S(1)} %fusion.5, bf16[2,128,256]{2,1,0:T(8,128)(2,1)S(1)} %get-tuple-element.12), kind=kOutput, calls=%fused_computation.2 | convolution fusion | flops 1213726720 | bytes 11075584 | tf_op jit(solution)/shard_map/bmk,bkr->bmr/dot_general | solution.py:79
  (17 shorter events, 0.2 us)
Async XLA Ops:
  0.0 109.4 %copy-start = (bf16[8192,128]{1,0:T(8,128)(2,1)S(1)}, bf16[8192,128]{1,0:T(8,128)(2,1)}, u32[]{:S(2)}) copy-start(bf16[8192,128]{1,0:T(8,128)(2,1)} %param.9) | copy-start | bytes 6291460
  0.0 7.9 %copy-start.7 = (bf16[3,2,128,256]{3,2,1,0:T(8,128)(2,1)S(1)}, bf16[3,2,128,256]{3,2,1,0:T(8,128)(2,1)}, u32[]{:S(2)}) copy-start(bf16[3,2,128,256]{3,2,1,0:T(8,128)(2,1)} %param.7) | copy-start | bytes 1179652
  5.0 2.8 %collective-permute-start = (bf16[2,128,2048]{2,1,0:T(8,128)(2,1)S(1)}, bf16[2,128,2048]{2,1,0:T(8,128)(2,1)S(1)}, u32[]{:S(2)}, u32[]{:S(2)}) collective-permute-start(bf16[2,128,2048]{2,1,0:T(8,128)(2,1)S(1)} %convolution_convert_fusion.7), channel_id=1, source_target_pairs={{0,4},{4,0},{8,12},{12,8},{16,20},{20,16},{24,28},{28,24},{1,5},{5... | collective-permute-start | bytes 3145736 | tf_op jit(solution)/shard_map/ppermute | solution.py:16
  8.3 26.4 %collective-permute-start.1 = (bf16[2,128,2048]{2,1,0:T(8,128)(2,1)S(1)}, bf16[2,128,2048]{2,1,0:T(8,128)(2,1)S(1)}, u32[]{:S(2)}, u32[]{:S(2)}) collective-permute-start(bf16[2,128,2048]{2,1,0:T(8,128)(2,1)S(1)} %fusion.10), channel_id=1, source_target_pairs={{0,8},{8,0},{4,12},{12,4},{16,24},{24,16},{20,28},{28,20},{1,9},{9... | collective-permute-start | bytes 3145736 | tf_op jit(solution)/shard_map/ppermute | solution.py:16
  35.2 24.7 %collective-permute-start.2 = (bf16[2,128,2048]{2,1,0:T(8,128)(2,1)S(1)}, bf16[2,128,2048]{2,1,0:T(8,128)(2,1)S(1)}, u32[]{:S(2)}, u32[]{:S(2)}) collective-permute-start(bf16[2,128,2048]{2,1,0:T(8,128)(2,1)S(1)} %fusion.11), channel_id=1, source_target_pairs={{0,16},{16,0},{4,20},{20,4},{8,24},{24,8},{12,28},{28,12},{1,17},{... | collective-permute-start | bytes 3145736 | tf_op jit(solution)/shard_map/ppermute | solution.py:16
  62.0 29.2 %all-to-all-start = ((bf16[4,2,128,512]{2,3,1,0:T(8,128)(2,1)}), bf16[4,2,128,512]{2,3,1,0:T(8,128)(2,1)S(1)}, u32[]{:S(2)}, u32[]{:S(2)}) async-start(bf16[4,2,128,512]{2,3,1,0:T(8,128)(2,1)} %pad_maximum_fusion), calls=%async_computation | async-start | bytes 2097152 | tf_op jit(solution)/shard_map/all_to_all | solution.py:60
  93.5 2.4 %copy-start.4 = (bf16[8,128,512]{2,1,0:T(8,128)(2,1)S(1)}, bf16[8,128,512]{2,1,0:T(8,128)(2,1)}, u32[]{:S(2)}) copy-start(bf16[8,128,512]{2,1,0:T(8,128)(2,1)} %copy.8) | copy-start | bytes 3145732
  98.7 2.4 %copy-start.5 = (bf16[8,512,128]{1,2,0:T(8,128)(2,1)S(1)}, bf16[8,512,128]{1,2,0:T(8,128)(2,1)}, u32[]{:S(2)}) copy-start(bf16[8,512,128]{1,2,0:T(8,128)(2,1)} %fusion.42) | copy-start | bytes 3145732
  103.9 2.4 %copy-start.6 = (bf16[8,512,128]{1,2,0:T(8,128)(2,1)S(1)}, bf16[8,512,128]{1,2,0:T(8,128)(2,1)}, u32[]{:S(2)}) copy-start(bf16[8,512,128]{1,2,0:T(8,128)(2,1)} %fusion.39) | copy-start | bytes 3145732
  119.8 2.8 %copy-start.3 = (bf16[8,128,256]{2,1,0:T(8,128)(2,1)S(1)}, bf16[8,128,256]{2,1,0:T(8,128)(2,1)}, u32[]{:S(2)}) copy-start(bf16[8,128,256]{2,1,0:T(8,128)(2,1)} %get-tuple-element.7) | copy-start | bytes 1572868
  121.6 1.0 copy-start.1
  124.0 2.1 copy-start.2
  132.6 28.8 %all-to-all-start.1 = ((bf16[8,128,512]{1,2,0:T(8,128)(2,1)}), bf16[8,128,512]{1,2,0:T(8,128)(2,1)S(1)}, u32[]{:S(2)}, u32[]{:S(2)}) async-start(bf16[8,128,512]{1,2,0:T(8,128)(2,1)} %fusion.33), calls=%async_computation.1 | async-start | bytes 2097152 | tf_op jit(solution)/shard_map/all_to_all | solution.py:75
  161.8 24.2 %collective-permute-start.3 = (bf16[2,128,2048]{1,2,0:T(8,128)(2,1)S(1)}, bf16[2,128,2048]{1,2,0:T(8,128)(2,1)S(1)}, u32[]{:S(2)}, u32[]{:S(2)}) collective-permute-start(bf16[2,128,2048]{1,2,0:T(8,128)(2,1)S(1)} %fusion.6), channel_id=1, source_target_pairs={{0,16},{16,0},{4,20},{20,4},{8,24},{24,8},{12,28},{28,12},{1,17},{... | collective-permute-start | bytes 3145736 | tf_op jit(solution)/shard_map/ppermute | solution.py:16
  186.9 23.4 %collective-permute-start.4 = (bf16[2,128,2048]{1,2,0:T(8,128)(2,1)S(1)}, bf16[2,128,2048]{1,2,0:T(8,128)(2,1)S(1)}, u32[]{:S(2)}, u32[]{:S(2)}) collective-permute-start(bf16[2,128,2048]{1,2,0:T(8,128)(2,1)S(1)} %fusion.7), channel_id=1, source_target_pairs={{0,8},{8,0},{4,12},{12,4},{16,24},{24,16},{20,28},{28,20},{1,9},{9... | collective-permute-start | bytes 3145736 | tf_op jit(solution)/shard_map/ppermute | solution.py:16
  211.2 2.9 %collective-permute-start.5 = (bf16[2,128,2048]{2,1,0:T(8,128)(2,1)S(1)}, bf16[2,128,2048]{2,1,0:T(8,128)(2,1)}, u32[]{:S(2)}, u32[]{:S(2)}) collective-permute-start(bf16[2,128,2048]{2,1,0:T(8,128)(2,1)S(1)} %fusion.8), channel_id=1, source_target_pairs={{0,4},{4,0},{8,12},{12,8},{16,20},{20,16},{24,28},{28,24},{1,5},{5... | collective-permute-start | bytes 3145736 | tf_op jit(solution)/shard_map/ppermute | solution.py:16
